TPU v7x, 32 devices: a whole 2x2x4 slice. The times are simulated.
32 devices in a mesh: groups: 2 (over y), seq: 4 (over z), head: 4 (over x, core).
Axes of the slice: x: 2, y: 2, z: 4, core: 2. Of those that a mesh axis runs over, the one named last changes fastest.
Arguments:
- residual: bfloat16 [4096, 2560], P(('groups', 'seq'), 'head'), parts along dimension 0, may hold values from -6 to 6
- x_in: bfloat16 [4096, 5120], P(('groups', 'seq'), 'head'), parts along dimension 0, may hold values from -6 to 6
- bc_in: bfloat16 [4096, 256], P(('groups', 'seq')), parts along dimension 0, may hold values from -1.5 to 1.5
- z_in: bfloat16 [4096, 5120], P(('groups', 'seq'), 'head'), parts along dimension 0, may hold values from -6 to 6
- dt_raw: float32 [80, 4096], P('head', ('groups', 'seq')), parts along dimension 1, may hold values from -5 to 5
- dt_bias: float32 [80], P('head'), may hold values from -3 to 0
- decay_rate: float32 [80], P('head'), may hold values from 0.0003 to 0.15
- d_skip: float32 [80], P('head'), may hold values from 1 to 4
- conv_x_weight: bfloat16 [4, 5120], P(None, 'head'), may hold values from -3 to 3
- conv_x_bias: bfloat16 [5120], P('head'), may hold values from -3 to 3
- conv_bc_weight: bfloat16 [4, 256], replicated, may hold values from -3 to 3
- conv_bc_bias: bfloat16 [256], replicated, may hold values from -3 to 3
- norm_gain: bfloat16 [5120], P('head'), may hold values from 0.5 to 1.5
- out_weight: bfloat16 [5120, 2560], P('head'), may hold values from -0.078125 to 0.078125
- final_gain: bfloat16 [2560], replicated, may hold values from 0.5 to 1.5
- lm_weight: bfloat16 [2560, 25600], P('seq', 'head'), may hold values from -15.811388 to 15.811388
- targets: int32 [4096], P(('groups', 'seq')), parts along dimension 0, may hold values from 0 to 25599
- doc_lengths: int32 [8], P('groups'), parts along dimension 0, may hold values from 1 to 1536, as said below
Outputs:
- block_out: bfloat16 [4096, 2560], P(('groups', 'seq'), 'head'), parts along dimension 0
- doc_loss: float32 [8], P('groups'), parts along dimension 0
There are 2 independent parts, one for each index of `groups`. A program takes and returns all parts, laid end to end along the dimension named above; an argument that names none is the same for every part. Nothing has to cross between parts.
Inputs may be any that keep to these rules, and one draw needn't show every extreme that they name: `doc_lengths`: the lengths of a group's 4 documents, in the order in which they are packed into its 2048 tokens; they sum to 2048.
All inputs are finite; a program needn't handle non-finite values.
Results may differ from a plain program's by a relative error of at most 0.00145.
The roundings to bfloat16 on the way count: a program that leaves them out, or rounds other values in their place, can miss the bound.
Values may be sent and summed in bfloat16 or wider, within the bound.
A program may use at most 128 MiB of HBM per device.

v0:
```python
import jax
import jax.numpy as jnp
from jax import lax
from jax.sharding import PartitionSpec as P

D = 2560
HEAD_SIZE = 64
STATE = 128
KERNEL = 4
SPAN = 256
INNER = 5120
EPSILON = 1e-05
HIGH = lax.Precision.HIGHEST


def shifted(array, axis, by):
    length = lax.axis_size(axis)
    pairs = [(i, i + by) for i in range(length) if 0 <= i + by < length]
    return lax.ppermute(array, axis, pairs)


def entering(part, axis, combine, identity):
    place = lax.axis_index(axis)
    gathered = jax.tree.map(lambda a: lax.all_gather(a, axis), part)
    state = jax.tree.map(lambda a, e: jnp.zeros_like(a) + jnp.asarray(e, a.dtype), part, identity)

    def one(lap, state):
        return combine(
            state, jax.tree.map(lambda a: lax.dynamic_index_in_dim(a, lap, 0, False), gathered)
        )

    return lax.fori_loop(0, place, one, state)


def merged(value, axis, join):
    pieces = jax.tree.map(lambda part: lax.all_gather(part, axis), value)
    head = jax.tree.map(lambda part: part[0], pieces)
    tail = jax.tree.map(lambda part: part[1:], pieces)
    running, _ = lax.scan(lambda running, section: (join(running, section), None), head, tail)
    return running


def document_of(positions, doc_lengths):
    starts = jnp.cumsum(doc_lengths) - doc_lengths
    return jnp.sum((positions[:, None] >= starts[None, :]).astype(jnp.int32), axis=1) - 1


def causal_conv(signal, rim_rows, weight, bias, positions, doc_ids, doc_lengths):
    length = signal.shape[0]
    taps = weight.shape[0]
    joined = jnp.concatenate([rim_rows, signal], axis=0).astype(jnp.float32)
    total = jnp.zeros(signal.shape, jnp.float32) + bias.astype(jnp.float32)[None, :]
    for offset in range(taps):
        lag = taps - 1 - offset
        source = document_of(positions - lag, doc_lengths)
        same = (source == doc_ids).astype(jnp.float32)
        total = (
            total
            + weight[offset].astype(jnp.float32)[None, :]
            * joined[offset : offset + length]
            * same[:, None]
        )
    return jax.nn.silu(total).astype(jnp.bfloat16)


def span_step(state, pieces, rates):
    signal, bmat, cmat, steps, doc_ids, doc_prev = pieces
    signal = signal.astype(jnp.float32)
    bmat = bmat.astype(jnp.float32)
    cmat = cmat.astype(jnp.float32)
    climb = jnp.cumsum(steps * rates[:, None], axis=1)
    extent = doc_ids.shape[0]
    order = jnp.arange(extent, dtype=jnp.int32)
    inside = (doc_ids[:, None] == doc_ids[None, :]) & (order[:, None] >= order[None, :])
    gap = climb[:, :, None] - climb[:, None, :]
    decay = jnp.where(inside[None], jnp.exp(-jnp.where(inside[None], gap, 0.0)), 0.0)
    scores = jnp.dot(cmat, bmat.T, precision=HIGH)
    weights = decay * scores[None] * steps[:, None, :]
    output = jnp.einsum("hts,shp->thp", weights, signal, precision=HIGH)
    carried = (doc_ids == doc_prev).astype(jnp.float32)
    entry = jnp.exp(-climb) * carried[None, :]
    output = output + jnp.einsum("tn,hpn->thp", cmat, state, precision=HIGH) * entry.T[:, :, None]
    last = doc_ids[extent - 1]
    tail = (
        jnp.exp(climb - climb[:, extent - 1 :])
        * (doc_ids == last).astype(jnp.float32)[None, :]
        * steps
    )
    kept = jnp.exp(-climb[:, extent - 1]) * (last == doc_prev).astype(jnp.float32)
    fresh = jnp.einsum("hs,shp,sn->hpn", tail, signal, bmat, precision=HIGH)
    return (kept[:, None, None] * state + fresh, output)


def chain_combine(earlier, later):
    return (earlier[0] * later[0], later[0][:, None, None] * earlier[1] + later[1])


def softmax_combine(first_part, second_part):
    peak = jnp.maximum(first_part[0], second_part[0])
    total = first_part[1] * jnp.exp(first_part[0] - peak) + second_part[1] * jnp.exp(
        second_part[0] - peak
    )
    return (peak, total, first_part[2] + second_part[2])


def local(
    residual,
    x_in,
    bc_in,
    z_in,
    dt_raw,
    dt_bias,
    decay_rate,
    d_skip,
    conv_x_weight,
    conv_x_bias,
    conv_bc_weight,
    conv_bc_bias,
    norm_gain,
    out_weight,
    final_gain,
    lm_weight,
    targets,
    doc_lengths,
):
    length = x_in.shape[0]
    inner_here = x_in.shape[1]
    heads_here = dt_raw.shape[0]
    seq_rank = lax.axis_index("seq")
    head_rank = lax.axis_index("head")
    offset_here = seq_rank * length
    positions = offset_here + jnp.arange(length, dtype=jnp.int32)
    doc_ids = document_of(positions, doc_lengths)
    margin = KERNEL - 1
    x_rim, bc_rim = shifted((x_in[length - margin :], bc_in[length - margin :]), "seq", 1)
    signal = causal_conv(x_in, x_rim, conv_x_weight, conv_x_bias, positions, doc_ids, doc_lengths)
    keys_queries = causal_conv(
        bc_in, bc_rim, conv_bc_weight, conv_bc_bias, positions, doc_ids, doc_lengths
    )
    steps = jax.nn.softplus(dt_raw + dt_bias[:, None])
    blocks = length // SPAN
    block_starts = offset_here + jnp.arange(blocks, dtype=jnp.int32) * SPAN
    pieces = (
        signal.reshape(blocks, SPAN, heads_here, HEAD_SIZE),
        keys_queries[:, :STATE].reshape(blocks, SPAN, STATE),
        keys_queries[:, STATE:].reshape(blocks, SPAN, STATE),
        steps.reshape(heads_here, blocks, SPAN).transpose(1, 0, 2),
        doc_ids.reshape(blocks, SPAN),
        document_of(block_starts - 1, doc_lengths),
    )

    def advance(state, piece):
        return span_step(state, piece, decay_rate)

    local_end, outputs = lax.scan(
        advance, jnp.zeros((heads_here, HEAD_SIZE, STATE), jnp.float32), pieces
    )
    outputs = outputs.reshape(length, heads_here, HEAD_SIZE)
    before = document_of(jnp.reshape(offset_here - 1, (1,)), doc_lengths)[0]
    carried = (doc_ids == before).astype(jnp.float32)
    climb = jnp.cumsum(steps * decay_rate[:, None], axis=1)
    through = jnp.exp(-climb[:, length - 1]) * carried[length - 1]
    identity = (jnp.ones_like(through), jnp.zeros_like(local_end))
    incoming = entering((through, local_end), "seq", chain_combine, identity)[1]
    entry = jnp.exp(-climb) * carried[None, :]
    cmat = keys_queries[:, STATE:].astype(jnp.float32)
    outputs = (
        outputs + jnp.einsum("tn,hpn->thp", cmat, incoming, precision=HIGH) * entry.T[:, :, None]
    )
    mixed = outputs + d_skip[None, :, None] * signal.reshape(length, heads_here, HEAD_SIZE).astype(
        jnp.float32
    )
    gated = mixed.reshape(length, inner_here) * jax.nn.silu(z_in.astype(jnp.float32))
    square_sum = lax.psum(jnp.sum(gated * gated, axis=1), "head")
    scale = lax.rsqrt(square_sum / INNER + EPSILON)
    normed = (gated * scale[:, None] * norm_gain.astype(jnp.float32)[None, :]).astype(jnp.bfloat16)
    partial_value = jnp.dot(normed, out_weight, preferred_element_type=jnp.float32)
    share = residual.shape[1]
    projected = lax.psum_scatter(partial_value, "head", scatter_dimension=1, tiled=True)
    block_out = (residual.astype(jnp.float32) + projected).astype(jnp.bfloat16)
    widened = block_out.astype(jnp.float32)
    square_total = lax.psum(jnp.sum(widened * widened, axis=1), "head")
    gain_part = lax.dynamic_slice_in_dim(final_gain, head_rank * share, share, 0)
    final_scale = lax.rsqrt(square_total / D + EPSILON)
    hidden_part = (widened * final_scale[:, None] * gain_part.astype(jnp.float32)[None, :]).astype(
        jnp.bfloat16
    )
    hidden = lax.all_gather(hidden_part, "head", axis=1, tiled=True)
    vocab_here = lm_weight.shape[1]
    logits = jnp.dot(
        hidden,
        lax.all_gather(lm_weight, "seq", axis=0, tiled=True),
        preferred_element_type=jnp.float32,
    )
    peak = jnp.max(logits, axis=1)
    total = jnp.sum(jnp.exp(logits - peak[:, None]), axis=1)
    local_target = targets - head_rank * vocab_here
    column = jnp.arange(vocab_here, dtype=jnp.int32)
    picked = jnp.sum(jnp.where(column[None, :] == local_target[:, None], logits, 0.0), axis=1)
    peak_all, total_all, picked_all = merged((peak, total, picked), "head", softmax_combine)
    losses = peak_all + jnp.log(total_all) - picked_all
    member = (
        doc_ids[:, None] == jnp.arange(doc_lengths.shape[0], dtype=jnp.int32)[None, :]
    ).astype(jnp.float32)
    sums = lax.psum(jnp.dot(losses, member, precision=HIGH), "seq")
    return (block_out, sums / doc_lengths.astype(jnp.float32))


def solution(mesh):
    in_specs = (
        P(("groups", "seq"), "head"),
        P(("groups", "seq"), "head"),
        P(("groups", "seq"), None),
        P(("groups", "seq"), "head"),
        P("head", ("groups", "seq")),
        P("head"),
        P("head"),
        P("head"),
        P(None, "head"),
        P("head"),
        P(),
        P(),
        P("head"),
        P("head", None),
        P(),
        P("seq", "head"),
        P(("groups", "seq")),
        P("groups"),
    )
    out_specs = (P(("groups", "seq"), "head"), P("groups"))
    return jax.shard_map(local, mesh=mesh, in_specs=in_specs, out_specs=out_specs, check_vma=False)
```

profile of v0, /device:TPU:0, one launch (start us, length us, event | category | flops | bytes accessed | tf_op | source)
XLA Modules:
  0.0 895.2 jit_solution(18207407152711681052)
XLA Ops:
  8.0 4.9 collective-permute-start
  13.7 3.5 collective-permute-start.1
  32.0 3.2 reshape.256
  35.5 83.1 %while.41 = (s32[]{:T(128)}, f32[20,64,128]{2,1,0:T(8,128)S(1)}, f32[2,256,20,64]{1,0,3,2:T(2,128)}, f32[2,20,256]{2,0,1:T(2,128)S(1)}, f32[20]{0:T(128)S(1)}, /...) while((s32[]{:T(128)}, f32[20,64,128]{2,1,0:T(8,128)S(1)}, ...), condition=%wide.region_9.10_spmd.clone, body=%wide.region_6.9_spmd.clone.sunk | while | flops 2040757376 | bytes 13968218 | solution.py:155
  39.0 4.2 fusion.119
  46.8 27.0 %dynamic_update_slice.6 = f32[2,256,20,64]{1,0,3,2:T(2,128)} dynamic-update-slice(f32[2,256,20,64]{1,0,3,2:T(2,128)} %get-tuple-element.469, f32[1,256,20,64]{1,0,3,2:T(1,128)S(1)} %copy.103, s32[]{:T(128)} %get-tuple-element.467, s32[]{:T(128)} %constant.109.clone.1..sunk.1, s32[]{:T(128)} %constant.109.clone.1..sunk.1, s32[]{:T(128)} %constant.109.clone.1..sunk.1) | dynamic-update-slice | bytes 2621444 | tf_op jit(solution)/shard_map/while/body/jit(dynamic_update_index_in_dim)/dynamic_update_slice | solution.py:155
  80.5 4.2 fusion.119
  88.3 27.0 %dynamic_update_slice.6 = f32[2,256,20,64]{1,0,3,2:T(2,128)} dynamic-update-slice(f32[2,256,20,64]{1,0,3,2:T(2,128)} %get-tuple-element.469, f32[1,256,20,64]{1,0,3,2:T(1,128)S(1)} %copy.103, s32[]{:T(128)} %get-tuple-element.467, s32[]{:T(128)} %constant.109.clone.1..sunk.1, s32[]{:T(128)} %constant.109.clone.1..sunk.1, s32[]{:T(128)} %constant.109.clone.1..sunk.1) | dynamic-update-slice | bytes 2621444 | tf_op jit(solution)/shard_map/while/body/jit(dynamic_update_index_in_dim)/dynamic_update_slice | solution.py:155
  126.1 11.2 %all-reduce = f32[80]{0:T(128)S(1)} all-reduce(f32[80]{0:T(128)S(1)} %dynamic-update-slice), channel_id=2, replica_groups=mesh['groups'=2,'seq'=4,'head'=4] {'seq'}, use_global_device_ids=true, to_apply=%add | all-reduce | flops 80 | bytes 640
  141.1 4.8 reshape.259
  145.8 27.9 %all-gather.16.cloned.1.call-done = f32[80,64,128]{2,1,0:T(8,128)} async-done(((f32[20,64,128]{2,1,0:T(8,128)}), f32[80,64,128]{2,1,0:T(8,128)}) %all-gather.16.cloned.1.call-update) | async-done | bytes 2621456 | tf_op jit(solution)/shard_map/all_gather | solution.py:24
  174.8 4.7 multiply_add_fusion.1
  183.8 6.3 psum.21
  190.1 9.7 %fusion.63 = f32[512,2560]{1,0:T(8,128)} fusion(bf16[1280,2560]{1,0:T(8,128)(2,1)} %param.37, f32[1280]{0:T(1024)S(1)} %convert_element_type.158, f32[512]{0:T(512)S(1)} %add_rsqrt_fusion.1, f32[512,1280]{1,0:T(8,128)S(1)} %copy.69, bf16[512,1280]{1,0:T(8,128)(2,1)} %param.27), kind=kOutput, calls=%fused_computation.95 | convolution fusion | flops 3361341440 | bytes 15735808 | tf_op jit(solution)/shard_map/dot_general | solution.py:177
  200.8 51.7 %reduce-scatter.2.cloned.1.call-done = f32[512,640]{1,0:T(8,128)} async-done(((f32[512,2560]{1,0:T(8,128)}), f32[512,640]{1,0:T(8,128)}) %reduce-scatter.2.cloned.1.call-update) | async-done | bytes 1310736 | tf_op jit(solution)/shard_map/reduce_scatter | solution.py:179
  254.1 5.8 psum.22
  261.6 25.6 %all-gather.12.cloned.1.call-done = bf16[512,2560]{1,0:T(8,128)(2,1)} async-done(((bf16[512,640]{1,0:T(8,128)(2,1)}), bf16[512,2560]{1,0:T(8,128)(2,1)}) %all-gather.12.cloned.1.call-update) | async-done | bytes 2621456 | tf_op jit(solution)/shard_map/all_gather | solution.py:188
  287.2 550.0 %all-gather.14.cloned.1.call-done = bf16[2560,6400]{1,0:T(8,128)(2,1)} async-done(((bf16[640,6400]{1,0:T(8,128)(2,1)}), bf16[2560,6400]{1,0:T(8,128)(2,1)}) %all-gather.14.cloned.1.call-update) | async-done | bytes 32768016 | tf_op jit(solution)/shard_map/all_gather | solution.py:192
  837.2 22.0 %fusion.89 = (f32[512]{0:T(512)S(1)}, f32[512,6400]{1,0:T(8,128)S(1)}) fusion(bf16[512,2560]{1,0:T(8,128)(2,1)} %all-gather.12.cloned.1.call-done, bf16[2560,6400]{1,0:T(8,128)(2,1)} %all-gather.14.cloned.1.call-done), kind=kOutput, calls=%fused_computation.167 | convolution fusion | flops 16780492800 | bytes 48498688 | tf_op jit(solution)/shard_map/dot_general | solution.py:190
  859.3 4.0 select_reduce_fusion
  863.3 5.2 all-gather.6
  868.5 5.2 all-gather.7
  873.7 5.2 all-gather.5
  879.5 8.6 psum.23
  (178 shorter events, 55.0 us)
Async XLA Ops:
  7.2 20.6 %copy-start.5 = (bf16[512,1280]{1,0:T(8,128)(2,1)S(1)}, bf16[512,1280]{1,0:T(8,128)(2,1)}, u32[]{:S(2)}) copy-start(bf16[512,1280]{1,0:T(8,128)(2,1)} %param.25) | copy-start | bytes 3932164
  7.2 166.6 %all-gather.16.cloned.1.call-start = ((), (), s32[]{:S(2)}) async-start(), calls=%async_computation.4 | async-start | bytes 3276800 | tf_op jit(solution)/shard_map/all_gather | solution.py:24
  8.0 19.7 %collective-permute-start = (bf16[3,1280]{1,0:T(4,128)(2,1)S(1)}, bf16[3,1280]{1,0:T(4,128)(2,1)S(1)}, u32[]{:S(2)}, u32[]{:S(2)}) collective-permute-start(bf16[3,1280]{1,0:T(4,128)(2,1)S(1)} %slice.106), channel_id=1, source_target_pairs={{0,4},{4,8},{8,12},{1,5},{5,9},{9,13},{2,6},{6,10},{10,14},{3,7},{... | collective-permute-start | bytes 23048 | tf_op jit(solution)/shard_map/ppermute | solution.py:19
  13.7 11.9 %collective-permute-start.1 = (bf16[3,256]{1,0:T(4,128)(2,1)S(1)}, bf16[3,256]{1,0:T(4,128)(2,1)S(1)}, u32[]{:S(2)}, u32[]{:S(2)}) collective-permute-start(bf16[3,256]{1,0:T(4,128)(2,1)S(1)} %slice.115), channel_id=1, source_target_pairs={{0,4},{4,8},{8,12},{1,5},{5,9},{9,13},{2,6},{6,10},{10,14},{3,7},{... | collective-permute-start | bytes 4616 | tf_op jit(solution)/shard_map/ppermute | solution.py:19
  20.9 7.1 copy-start.9
  27.0 1.0 copy-start.3
  30.5 1.5 copy-start.1
  32.0 3.4 copy-start.7
  35.5 3.5 copy-start.14
  46.7 30.2 %copy-start.8 = (f32[20]{0:T(128)S(1)}, f32[20]{0:T(128)}, u32[]{:S(2)}) copy-start(f32[20]{0:T(128)} %get-tuple-element.571) | copy-start | bytes 244 | tf_op jit(solution)/shard_map/while
  46.7 30.2 %copy-start.15 = (s32[2]{0:T(128)S(1)}, s32[2]{0:T(128)}, u32[]{:S(2)}) copy-start(s32[2]{0:T(128)} %copy-done.14) | copy-start | bytes 28 | tf_op jit(solution)/shard_map/while
  77.0 3.5 copy-start.14
  88.3 30.2 %copy-start.8 = (f32[20]{0:T(128)S(1)}, f32[20]{0:T(128)}, u32[]{:S(2)}) copy-start(f32[20]{0:T(128)} %get-tuple-element.571) | copy-start | bytes 244 | tf_op jit(solution)/shard_map/while
  88.3 30.2 %copy-start.15 = (s32[2]{0:T(128)S(1)}, s32[2]{0:T(128)}, u32[]{:S(2)}) copy-start(s32[2]{0:T(128)} %copy-done.14) | copy-start | bytes 28 | tf_op jit(solution)/shard_map/while
  118.5 0.8 copy-start
  119.4 133.1 %reduce-scatter.2.cloned.1.call-start = ((), (), s32[]{:S(2)}) async-start(), calls=%async_computation.1 | async-start | bytes 6553600 | tf_op jit(solution)/shard_map/reduce_scatter | solution.py:179
  173.8 1.0 copy-start.4
  173.8 0.9 copy-start.12
  199.9 52.6 %copy-start.6 = (bf16[512,640]{1,0:T(8,128)(2,1)S(1)}, bf16[512,640]{1,0:T(8,128)(2,1)}, u32[]{:S(2)}) copy-start(bf16[512,640]{1,0:T(8,128)(2,1)} %param.24) | copy-start | bytes 1966084
  199.9 87.4 %all-gather.12.cloned.1.call-start = ((), (), s32[]{:S(2)}) async-start(), calls=%async_computation.2 | async-start | bytes 3276800 | tf_op jit(solution)/shard_map/all_gather | solution.py:188
  254.1 7.5 copy-start.2
  260.9 576.3 %all-gather.14.cloned.1.call-start = ((), (), s32[]{:S(2)}) async-start(), calls=%async_computation.3 | async-start | bytes 40960000 | tf_op jit(solution)/shard_map/all_gather | solution.py:192
  859.3 19.9 %copy-start.10 = (s32[512]{0:T(512)S(1)}, s32[512]{0:T(512)}, u32[]{:S(2)}) copy-start(s32[512]{0:T(512)} %copy-done.9) | copy-start | bytes 6148
  859.3 28.8 %copy-start.13 = (s32[4]{0:T(128)S(1)}, s32[4]{0:T(128)}, u32[]{:S(2)}) copy-start(s32[4]{0:T(128)} %param.41) | copy-start | bytes 52
  (1 other events, 0.7 us)
Sparse Core Ops, SparseCore 0:
  119.5 54.1 all-gather.15
  200.0 52.4 reduce-scatter.1
  261.1 26.1 all-gather.11
  288.7 548.5 all-gather.13
where the time goes:
time: 900 us; the launch traced here: 895 us
  waiting for transfers between devices  656 us (73%)
  local copies, waits for them, and re-layouts  81.8 us (9%)
  matrix products  52.3 us (6%)
  blocking collectives  47.5 us (5%)
  other arithmetic  30.7 us (3%)
  between operations  15.5 us (2%)
    all_gather x1, waiting for transfers between devices, local(): lax.all_gather(lm_weight, 'seq', axis=0, tiled=True)  550 us
    dynamic_update_slice x4, local copies, waits for them, and re-layouts, local(): lax.scan(advance, jnp.zeros((heads_here, HEAD_SIZE, STATE), jnp.float32),...  56.8 us
    reduce_scatter x1, waiting for transfers between devices, local(): lax.psum_scatter(partial_value, 'head', scatter_dimension=1, tiled=True)  51.7 us
    all_gather x1, waiting for transfers between devices, entering(): gathered = jax.tree.map(lambda a: lax.all_gather(a, axis), part)  27.9 us
    all_gather x1, waiting for transfers between devices, local(): hidden = lax.all_gather(hidden_part, 'head', axis=1, tiled=True)  25.6 us
    dot_general x1, matrix products, local(): jnp.dot(hidden, lax.all_gather(lm_weight, 'seq', axis=0, tiled=True), pre...  22 us
  transfers between devices with their start and end apart: 6, of which 4 were waited for; matrix products, arithmetic and copies ran while one was open for 3% of the time, Pallas kernels for 0%

commit v1 on v0

--- a/solution.py
+++ b/solution.py
@@ -11,6 +11,13 @@
 INNER = 5120
 EPSILON = 1e-05
 HIGH = lax.Precision.HIGHEST
+
+
+def exchange_gather(array, name, along):
+    peers = lax.axis_size(name)
+    pieces = jnp.stack([array for _ in range(peers)])
+    pieces = lax.all_to_all(pieces, name, split_axis=0, concat_axis=0)
+    return jnp.concatenate(pieces, axis=along)
 
 
 def shifted(array, axis, by):
@@ -188,9 +195,7 @@
     hidden = lax.all_gather(hidden_part, "head", axis=1, tiled=True)
     vocab_here = lm_weight.shape[1]
     logits = jnp.dot(
-        hidden,
-        lax.all_gather(lm_weight, "seq", axis=0, tiled=True),
-        preferred_element_type=jnp.float32,
+        hidden, exchange_gather(lm_weight, "seq", 0), preferred_element_type=jnp.float32
     )
     peak = jnp.max(logits, axis=1)
     total = jnp.sum(jnp.exp(logits - peak[:, None]), axis=1)

time: 900 us -> 1070 us (1.19)
  blocking collectives: 47.5 us -> 226 us
  waiting for transfers between devices: 656 us -> 624 us
  local copies, waits for them, and re-layouts: 81.8 us -> 94.5 us
    all_gather x1 -> x0, waiting for transfers between devices: 550 us -> none  [local(): lax.all_gather(lm_weight, 'seq', axis=0, tiled=True)]
    ppermute x2, waiting for transfers between devices: 0.01 us -> 515 us  [shifted(): return lax.ppermute(array, axis, pairs)]
    unnamed x1, blocking collectives: 11.2 us -> 187 us
    another operation x10 -> x11, local copies, waits for them, and re-layouts: 1.11 us -> 14.3 us  [the longest x1 13.1 us: exchange_gather(): pieces = jnp.stack([array for _ in range(peers)])]
  transfers between devices with their start and end apart: 6 -> 6, of which waited for: 4 -> 4; matrix products, arithmetic and copies ran while one was open for 3% -> 12% of each run, Pallas kernels for 0% -> 0%
where the time goes in v1:
time: 1070 us; the launch traced here: 1060 us
  waiting for transfers between devices  624 us (58%)
  blocking collectives  226 us (21%)
  local copies, waits for them, and re-layouts  94.5 us (9%)
  matrix products  52.3 us (5%)
  other arithmetic  27.1 us (3%)
  starting transfers between devices  18.3 us (2%)
  between operations  15.6 us (1%)
    ppermute x2, waiting for transfers between devices, shifted(): return lax.ppermute(array, axis, pairs)  515 us
    unnamed x1, blocking collectives  187 us
    dynamic_update_slice x4, local copies, waits for them, and re-layouts, local(): lax.scan(advance, jnp.zeros((heads_here, HEAD_SIZE, STATE), jnp.float32),...  56.8 us
    reduce_scatter x1, waiting for transfers between devices, local(): lax.psum_scatter(partial_value, 'head', scatter_dimension=1, tiled=True)  51.6 us
    all_gather x1, waiting for transfers between devices, entering(): gathered = jax.tree.map(lambda a: lax.all_gather(a, axis), part)  31 us
    all_gather x1, waiting for transfers between devices, local(): hidden = lax.all_gather(hidden_part, 'head', axis=1, tiled=True)  26.3 us
    dot_general x1, matrix products, local(): jnp.dot(hidden, exchange_gather(lm_weight, 'seq', 0), preferred_element_t...  22 us
  transfers between devices with their start and end apart: 6, of which 4 were waited for; matrix products, arithmetic and copies ran while one was open for 12% of the time, Pallas kernels for 0%

profile of v1, /device:TPU:0, one launch (start us, length us, event | category | flops | bytes accessed | tf_op | source)
XLA Modules:
  0.0 1060.7 jit_solution(8223033496674715499)
XLA Ops:
  7.2 13.1 %stack.2 = bf16[4,640,6400]{2,1,0:T(8,128)(2,1)} broadcast(bf16[640,6400]{1,0:T(8,128)(2,1)} %param.39), dimensions={1,2} | broadcast | bytes 40960000 | tf_op jit(solution)/shard_map/stack | solution.py:18
  20.4 9.7 all-to-all-start
  30.2 5.0 collective-permute-start
  43.2 514.9 %collective-permute-done.1 = bf16[3,256]{1,0:T(4,128)(2,1)S(1)} collective-permute-done((bf16[3,256]{1,0:T(4,128)(2,1)S(1)}, bf16[3,256]{1,0:T(4,128)(2,1)S(1)}, u32[]{:S(2)}, u32[]{:S(2)}) %collective-permute-start.1) | collective-permute-done | bytes 1568 | tf_op jit(solution)/shard_map/ppermute | solution.py:26
  567.2 85.5 %while.41 = (s32[]{:T(128)}, f32[20,64,128]{2,1,0:T(8,128)S(1)}, f32[2,256,20,64]{1,0,3,2:T(2,128)}, f32[2,20,256]{2,0,1:T(2,128)S(1)}, f32[20]{0:T(128)}, /*ind...) while((s32[]{:T(128)}, f32[20,64,128]{2,1,0:T(8,128)S(1)}, ...), condition=%wide.region_9.10_spmd.clone, body=%wide.region_6.9_spmd.clone.sunk | while | flops 2040757376 | bytes 13967742 | solution.py:162
  571.9 4.2 fusion.119
  579.8 27.0 %dynamic_update_slice.6 = f32[2,256,20,64]{1,0,3,2:T(2,128)} dynamic-update-slice(f32[2,256,20,64]{1,0,3,2:T(2,128)} %get-tuple-element.469, f32[1,256,20,64]{1,0,3,2:T(1,128)S(1)} %copy.103, s32[]{:T(128)} %get-tuple-element.467, s32[]{:T(128)} %constant.109.clone.1..sunk.1, s32[]{:T(128)} %constant.109.clone.1..sunk.1, s32[]{:T(128)} %constant.109.clone.1..sunk.1) | dynamic-update-slice | bytes 2621444 | tf_op jit(solution)/shard_map/while/body/jit(dynamic_update_index_in_dim)/dynamic_update_slice | solution.py:162
  614.6 4.2 fusion.119
  622.5 27.0 %dynamic_update_slice.6 = f32[2,256,20,64]{1,0,3,2:T(2,128)} dynamic-update-slice(f32[2,256,20,64]{1,0,3,2:T(2,128)} %get-tuple-element.469, f32[1,256,20,64]{1,0,3,2:T(1,128)S(1)} %copy.103, s32[]{:T(128)} %get-tuple-element.467, s32[]{:T(128)} %constant.109.clone.1..sunk.1, s32[]{:T(128)} %constant.109.clone.1..sunk.1, s32[]{:T(128)} %constant.109.clone.1..sunk.1) | dynamic-update-slice | bytes 2621444 | tf_op jit(solution)/shard_map/while/body/jit(dynamic_update_index_in_dim)/dynamic_update_slice | solution.py:162
  660.1 186.7 %all-reduce = f32[80]{0:T(128)S(1)} all-reduce(f32[80]{0:T(128)S(1)} %dynamic-update-slice), channel_id=2, replica_groups=mesh['groups'=2,'seq'=4,'head'=4] {'seq'}, use_global_device_ids=true, to_apply=%add | all-reduce | flops 80 | bytes 640
  850.5 4.7 reshape.264
  855.2 31.0 %all-gather.13.cloned.1.call-done = f32[80,64,128]{2,1,0:T(8,128)} async-done(((f32[20,64,128]{2,1,0:T(8,128)}), f32[80,64,128]{2,1,0:T(8,128)}) %all-gather.13.cloned.1.call-update) | async-done | bytes 2621456 | tf_op jit(solution)/shard_map/all_gather | solution.py:31
  887.3 4.7 multiply_add_fusion.1
  896.3 6.4 psum.21
  902.7 9.7 fusion.63
  913.3 51.6 %reduce-scatter.2.cloned.1.call-done = f32[512,640]{1,0:T(8,128)} async-done(((f32[512,2560]{1,0:T(8,128)}), f32[512,640]{1,0:T(8,128)}) %reduce-scatter.2.cloned.1.call-update) | async-done | bytes 1310736 | tf_op jit(solution)/shard_map/reduce_scatter | solution.py:186
  966.5 5.8 psum.22
  973.4 26.3 %all-gather.11.cloned.1.call-done = bf16[512,2560]{1,0:T(8,128)(2,1)} async-done(((bf16[512,640]{1,0:T(8,128)(2,1)}), bf16[512,2560]{1,0:T(8,128)(2,1)}) %all-gather.11.cloned.1.call-update) | async-done | bytes 2621456 | tf_op jit(solution)/shard_map/all_gather | solution.py:195
  999.7 22.0 %fusion.89 = (f32[512]{0:T(512)S(1)}, f32[512,6400]{1,0:T(8,128)S(1)}) fusion(bf16[512,2560]{1,0:T(8,128)(2,1)} %all-gather.11.cloned.1.call-done, bf16[2560,6400]{1,0:T(8,128)(2,1)} %bitcast.21), kind=kOutput, calls=%fused_computation.167 | convolution fusion | flops 16780492800 | bytes 48498688 | tf_op jit(solution)/shard_map/dot_general | solution.py:197
  1021.8 4.0 select_reduce_fusion
  1025.8 5.2 all-gather.6
  1031.0 5.2 all-gather.7
  1036.2 5.2 all-gather.5
  1041.9 11.7 %psum.23 = f32[4]{0:T(128)S(1)} all-reduce(f32[4]{0:T(128)S(1)} %convolution_bitcast_fusion), channel_id=1, replica_groups=mesh['groups'=2,'seq'=4,'head'=4] {'seq'}, use_global_device_ids=true, to_apply=%region_25.26 | all-reduce | flops 4 | bytes 32 | tf_op jit(solution)/shard_map/psum | solution.py:210
  (180 shorter events, 57.2 us)
Async XLA Ops:
  20.3 9.9 copy-start.5
  20.3 14.9 %copy-start.7 = (bf16[512,256]{1,0:T(8,128)(2,1)S(1)}, bf16[512,256]{1,0:T(8,128)(2,1)}, u32[]{:S(2)}) copy-start(bf16[512,256]{1,0:T(8,128)(2,1)} %param.26) | copy-start | bytes 786436
  20.3 18.4 %copy-start.17 = (s32[4]{0:T(128)S(1)}, s32[4]{0:T(128)}, u32[]{:S(2)}) copy-start(s32[4]{0:T(128)} %param.41) | copy-start | bytes 52
  20.3 20.8 %copy-start.10 = (bf16[4,256]{1,0:T(4,128)(2,1)S(1)}, bf16[4,256]{1,0:T(4,128)(2,1)}, u32[]{:S(2)}) copy-start(bf16[4,256]{1,0:T(4,128)(2,1)} %param.34) | copy-start | bytes 6148
  20.3 21.4 %copy-start.8 = (f32[20,512]{1,0:T(8,128)S(1)}, f32[20,512]{1,0:T(8,128)}, u32[]{:S(2)}) copy-start(f32[20,512]{1,0:T(8,128)} %param.28) | copy-start | bytes 122884
  20.3 21.4 %copy-start.15 = (f32[20]{0:T(128)S(1)}, f32[20]{0:T(128)}, u32[]{:S(2)}) copy-start(f32[20]{0:T(128)} %param.29) | copy-start | bytes 244
  20.4 22.7 %copy-start.9 = (bf16[4,1280]{1,0:T(4,128)(2,1)S(1)}, bf16[4,1280]{1,0:T(4,128)(2,1)}, u32[]{:S(2)}) copy-start(bf16[4,1280]{1,0:T(4,128)(2,1)} %param.32) | copy-start | bytes 30724
  20.4 22.8 %copy-start.13 = (bf16[1280]{0:T(1024)(128)(2,1)S(1)}, bf16[1280]{0:T(1024)(128)(2,1)}, u32[]{:S(2)}) copy-start(bf16[1280]{0:T(1024)(128)(2,1)} %param.33) | copy-start | bytes 7684
  20.4 22.8 %copy-start.19 = (bf16[256]{0:T(256)(128)(2,1)S(1)}, bf16[256]{0:T(256)(128)(2,1)}, u32[]{:S(2)}) copy-start(bf16[256]{0:T(256)(128)(2,1)} %param.35) | copy-start | bytes 1540
  20.4 979.3 %all-to-all-start = ((bf16[4,640,6400]{2,1,0:T(8,128)(2,1)}), bf16[4,640,6400]{2,1,0:T(8,128)(2,1)}, u32[]{:S(2)}, u32[]{:S(2)}) async-start(bf16[4,640,6400]{2,1,0:T(8,128)(2,1)} %stack.2), calls=%async_computation.1 | async-start | bytes 65536000 | tf_op jit(solution)/shard_map/all_to_all | solution.py:19
  30.1 856.1 %all-gather.13.cloned.1.call-start = ((), (), s32[]{:S(2)}) async-start(), calls=%async_computation.4 | async-start | bytes 3276800 | tf_op jit(solution)/shard_map/all_gather | solution.py:31
  30.2 529.2 %collective-permute-start = (bf16[3,1280]{1,0:T(4,128)(2,1)S(1)}, bf16[3,1280]{1,0:T(4,128)(2,1)S(1)}, u32[]{:S(2)}, u32[]{:S(2)}) collective-permute-start(bf16[3,1280]{1,0:T(4,128)(2,1)S(1)} %slice.106), channel_id=1, source_target_pairs={{0,4},{4,8},{8,12},{1,5},{5,9},{9,13},{2,6},{6,10},{10,14},{3,7},{... | collective-permute-start | bytes 23048 | tf_op jit(solution)/shard_map/ppermute | solution.py:26
  35.2 522.9 %collective-permute-start.1 = (bf16[3,256]{1,0:T(4,128)(2,1)S(1)}, bf16[3,256]{1,0:T(4,128)(2,1)S(1)}, u32[]{:S(2)}, u32[]{:S(2)}) collective-permute-start(bf16[3,256]{1,0:T(4,128)(2,1)S(1)} %slice.115), channel_id=1, source_target_pairs={{0,4},{4,8},{8,12},{1,5},{5,9},{9,13},{2,6},{6,10},{10,14},{3,7},{... | collective-permute-start | bytes 4616 | tf_op jit(solution)/shard_map/ppermute | solution.py:26
  41.1 518.6 %copy-start.11 = (s32[512]{0:T(512)}, s32[512]{0:T(512)S(1)}, u32[]{:S(2)}) copy-start(s32[512]{0:T(512)S(1)} %broadcast_add_fusion.2) | copy-start | bytes 6148
  558.6 1.0 copy-start.3
  562.3 1.5 copy-start.1
  653.6 311.4 %reduce-scatter.2.cloned.1.call-start = ((), (), s32[]{:S(2)}) async-start(), calls=%async_computation.2 | async-start | bytes 6553600 | tf_op jit(solution)/shard_map/reduce_scatter | solution.py:186
  886.3 1.0 copy-start.4
  912.4 52.5 %copy-start.6 = (bf16[512,640]{1,0:T(8,128)(2,1)S(1)}, bf16[512,640]{1,0:T(8,128)(2,1)}, u32[]{:S(2)}) copy-start(bf16[512,640]{1,0:T(8,128)(2,1)} %param.24) | copy-start | bytes 1966084
  912.5 61.0 %copy-start.14 = (s32[512]{0:T(512)S(1)}, s32[512]{0:T(512)}, u32[]{:S(2)}) copy-start(s32[512]{0:T(512)} %param.40) | copy-start | bytes 6148
  912.5 87.3 %all-gather.11.cloned.1.call-start = ((), (), s32[]{:S(2)}) async-start(), calls=%async_computation.3 | async-start | bytes 3276800 | tf_op jit(solution)/shard_map/all_gather | solution.py:195
  966.5 55.2 %copy-start.2 = (bf16[512,640]{1,0:T(8,128)(2,1)}, bf16[512,640]{1,0:T(8,128)(2,1)S(1)}, u32[]{:S(2)}) copy-start(bf16[512,640]{1,0:T(8,128)(2,1)S(1)} %get-tuple-element.276) | copy-start | bytes 1966084
  1021.7 19.9 %copy-start.12 = (s32[512]{0:T(512)S(1)}, s32[512]{0:T(512)}, u32[]{:S(2)}) copy-start(s32[512]{0:T(512)} %copy-done.11) | copy-start | bytes 6148
  1021.7 31.9 %copy-start.18 = (s32[4]{0:T(128)S(1)}, s32[4]{0:T(128)}, u32[]{:S(2)}) copy-start(s32[4]{0:T(128)} %param.41) | copy-start | bytes 52
  (2 other events, 1.8 us)
Sparse Core Ops, SparseCore 0:
  653.7 232.5 all-gather.12
  912.6 52.3 reduce-scatter.1
  973.5 26.1 all-gather.10
